TPU v7x, 8 devices: a whole 2x2x1 slice. The times are simulated.
8 devices in a mesh: dp: 1 (over z), ep: 8 (over x, y, core).
Axes of the slice: x: 2, y: 2, z: 1, core: 2. Of those that a mesh axis runs over, the one named last changes fastest.
Arguments:
- x: bfloat16 [1, 8, 256, 3072], P('dp', 'ep')
- expert: int32 [1, 8, 256, 4], P('dp', 'ep')
- slot: int32 [1, 8, 256, 4], P('dp', 'ep')
- gate: float32 [1, 8, 256, 4], P('dp', 'ep')
- w_gate: bfloat16 [16, 3072, 10752], P('ep')
- w_up: bfloat16 [16, 3072, 10752], P('ep')
- w_down: bfloat16 [16, 10752, 3072], P('ep')
Outputs:
- y: bfloat16 [1, 8, 256, 3072], P('dp', 'ep')
All inputs are finite; a program needn't handle non-finite values.
Results may differ from a plain program's by a relative error of at most 0.009.
Values are sent between devices in bfloat16 or wider.
A program may use at most 2 GiB of HBM per device.

v0:
```python
import jax
import jax.numpy as jnp
from jax import lax
from jax.sharding import NamedSharding, PartitionSpec as P


def einsum(form, a, b):
    return jnp.einsum(form, a.astype(jnp.float32), b.astype(jnp.float32))


def solution(mesh):
    def placed(v, *spec):
        return lax.with_sharding_constraint(v, NamedSharding(mesh, P(*spec)))

    def step(x, expert, slot, gate, w_gate, w_up, w_down):
        experts, (tokens, top) = w_gate.shape[0], expert.shape[2:]
        slots = 5 * tokens * top // (4 * experts)
        to_expert = jax.nn.one_hot(expert, experts, dtype=jnp.bfloat16)
        to_slot = jax.nn.one_hot(slot, slots, dtype=jnp.bfloat16)
        weighted = to_expert * gate[..., None].astype(jnp.bfloat16)
        dispatch = einsum("abtke,abtkc->abtec", to_expert, to_slot).astype(jnp.bfloat16)
        combine = einsum("abtke,abtkc->abtec", weighted, to_slot).astype(jnp.bfloat16)
        z = einsum("abtec,abtd->aebcd", dispatch, x).astype(jnp.bfloat16)
        z = placed(z, "dp", None, "ep", None, None)
        z = placed(z, "dp", "ep", None, None, None)
        h = jax.nn.silu(einsum("aebcd,edf->aebcf", z, w_gate))
        h = (h * einsum("aebcd,edf->aebcf", z, w_up)).astype(jnp.bfloat16)
        out = einsum("aebcf,efd->aebcd", h, w_down).astype(jnp.bfloat16)
        out = placed(out, "dp", "ep", None, None, None)
        out = placed(out, "dp", None, "ep", None, None)
        y = einsum("abtec,aebcd->abtd", combine, out)
        return y.astype(jnp.bfloat16)

    return step
```

profile of v0, /device:TPU:0, one launch (start us, length us, event | category | flops | bytes accessed | tf_op | source)
XLA Modules:
  0.0 497.4 jit_solution(14299515479352427455)
XLA Ops:
  0.0 0.0 copy-start
  0.0 0.9 copy.11
  0.9 0.0 copy-start.3
  1.0 0.8 copy.9
  1.8 0.0 copy-start.5
  1.8 2.0 convolution_convert_fusion.2
  3.8 0.0 copy-done
  3.8 2.3 convolution_convert_fusion
  6.2 91.8 %all-to-all.4 = bf16[1,8,2,1,80,3072]{5,4,2,3,0,1:T(8,128)(2,1)S(1)} all-to-all(bf16[1,8,2,1,80,3072]{5,4,2,3,0,1:T(8,128)(2,1)S(1)} %bitcast.108), channel_id=1, replica_groups=mesh['dp'=1,'ep'=8] {'ep'}, dimensions={1} | all-to-all | bytes 15728640 | tf_op jit(solution)/sharding_constraint;jit(solution)/sharding_constraint | solution.py:13
  97.9 0.0 copy-start.2
  97.9 3.1 copy-done.2
  101.1 94.0 %fusion.2 = f32[2,8,80,10752]{3,2,1,0:T(8,128)} fusion(bf16[2,3072,10752]{2,1,0:T(8,128)(2,1)} %param.5, bf16[1,8,2,1,80,3072]{5,4,2,3,0,1:T(8,128)(2,1)S(1)} %all-to-all.4), kind=kOutput, calls=%fused_computation.2 | convolution fusion | flops 84557168640 | bytes 195035136 | tf_op jit(solution)/aebcd,edf->aebcf/dot_general | solution.py:8
  195.1 0.0 copy-done.3
  195.1 0.0 copy-done.5
  195.1 100.5 %fusion.6 = bf16[1,2,8,80,10752]{4,3,2,1,0:T(8,128)(2,1)} fusion(f32[2,8,80,10752]{3,2,1,0:T(8,128)} %fusion.2, bf16[2,3072,10752]{2,1,0:T(8,128)(2,1)} %param.4, bf16[1,8,2,1,80,3072]{5,4,2,3,0,1:T(8,128)(2,1)} %copy-done.2), kind=kOutput, calls=%fused_computation.7 | convolution fusion | flops 84639744000 | bytes 222560256 | tf_op jit(solution)/aebcd,edf->aebcf/dot_general | solution.py:8
  295.6 96.5 %convert_bitcast_fusion = bf16[1,2,8,1,80,3072]{5,4,2,1,3,0:T(8,128)(2,1)} fusion(bf16[2,10752,3072]{2,1,0:T(8,128)(2,1)} %param.6, bf16[1,2,8,80,10752]{4,3,2,1,0:T(8,128)(2,1)} %fusion.6), kind=kOutput, calls=%fused_computation.16 | convolution fusion | flops 84561100800 | bytes 167510016 | tf_op jit(solution)/aebcf,efd->aebcd/dot_general | solution.py:8
  392.0 0.0 copy-start.7
  392.1 0.0 copy-start.4
  392.1 0.0 copy-start.6
  392.1 7.2 %copy.15 = bf16[1,2,8,1,80,3072]{5,4,1,3,0,2:T(8,128)(2,1)} copy(bf16[1,2,8,1,80,3072]{5,4,2,1,3,0:T(8,128)(2,1)} %convert_bitcast_fusion) | data formatting | bytes 15728640 | tf_op jit(solution)/sharding_constraint;jit(solution)/sharding_constraint | solution.py:13
  399.3 3.7 all-to-all-start.1
  403.0 0.0 copy-done.7
  403.0 0.1 copy.10
  403.2 0.0 copy-done.4
  403.2 0.0 copy-done.6
  403.2 0.0 copy-start.1
  403.2 2.4 convolution_convert_fusion.1
  405.6 84.6 %all-to-all-done.1 = bf16[1,2,8,1,80,3072]{5,4,1,3,0,2:T(8,128)(2,1)} async-done(((bf16[1,2,8,1,80,3072]{5,4,1,3,0,2:T(8,128)(2,1)}), bf16[1,2,8,1,80,3072]{5,4,1,3,0,2:T(8,128)(2,1)}, u32[]{:S(2)}, u32[]{:S(2)}) %all-to-all-start.1) | async-done | bytes 7864352 | tf_op jit(solution)/sharding_constraint;jit(solution)/sharding_constraint | solution.py:13
  490.2 7.2 %fusion.22 = bf16[1,1,256,3072]{3,2,1,0:T(8,128)(2,1)} fusion(bf16[16,80,3072]{2,1,0:T(8,128)(2,1)} %bitcast.38, bf16[256,16,80]{2,1,0:T(8,128)(2,1)S(1)} %convolution_convert_fusion.1), kind=kOutput, calls=%fused_computation.22 | convolution fusion | flops 2014052352 | bytes 10092544 | tf_op jit(solution)/abtec,aebcd->abtd/dot_general | solution.py:8
  497.4 0.0 copy-done.1
  (1 shorter events, 0.0 us)
Async XLA Ops:
  0.0 3.8 copy-start
  0.9 194.2 %copy-start.3 = (s32[256,4]{1,0:T(8,128)}, s32[256,4]{1,0:T(8,128)S(1)}, u32[]{:S(2)}) copy-start(s32[256,4]{1,0:T(8,128)S(1)} %copy.11) | copy-start | bytes 12292
  1.8 193.3 %copy-start.5 = (s32[256,4]{1,0:T(8,128)}, s32[256,4]{1,0:T(8,128)S(1)}, u32[]{:S(2)}) copy-start(s32[256,4]{1,0:T(8,128)S(1)} %copy.9) | copy-start | bytes 12292
  97.9 3.1 copy-start.2
  392.0 11.0 %copy-start.7 = (f32[1,1,256,4]{2,3,1,0:T(4,128)S(1)}, f32[1,1,256,4]{2,3,1,0:T(4,128)}, u32[]{:S(2)}) copy-start(f32[1,1,256,4]{2,3,1,0:T(4,128)} %param.1) | copy-start | bytes 12292
  392.1 11.1 %copy-start.4 = (s32[256,4]{1,0:T(8,128)S(1)}, s32[256,4]{1,0:T(8,128)}, u32[]{:S(2)}) copy-start(s32[256,4]{1,0:T(8,128)} %copy-done.3) | copy-start | bytes 12292
  392.1 11.1 %copy-start.6 = (s32[256,4]{1,0:T(8,128)S(1)}, s32[256,4]{1,0:T(8,128)}, u32[]{:S(2)}) copy-start(s32[256,4]{1,0:T(8,128)} %copy-done.5) | copy-start | bytes 12292
  399.3 90.9 %all-to-all-start.1 = ((bf16[1,2,8,1,80,3072]{5,4,1,3,0,2:T(8,128)(2,1)}), bf16[1,2,8,1,80,3072]{5,4,1,3,0,2:T(8,128)(2,1)}, u32[]{:S(2)}, u32[]{:S(2)}) async-start(bf16[1,2,8,1,80,3072]{5,4,1,3,0,2:T(8,128)(2,1)} %copy.15), calls=%async_computation.1 | async-start | bytes 15728640 | tf_op jit(solution)/sharding_constraint;jit(solution)/sharding_constraint | solution.py:13
  403.2 94.2 %copy-start.1 = (bf16[1,1,256,3072]{3,2,1,0:T(8,128)(2,1)S(1)}, bf16[1,1,256,3072]{3,2,1,0:T(8,128)(2,1)}, u32[]{:S(2)}) copy-start(bf16[1,1,256,3072]{3,2,1,0:T(8,128)(2,1)} %param.3) | copy-start | bytes 4718596
where the time goes:
time: 498 us; the launch traced here: 497 us
  matrix products  305 us (61%)
  blocking collectives  91.8 us (18%)
  waiting for transfers between devices  84.6 us (17%)
  local copies, waits for them, and re-layouts  12.3 us (2%)
    dot_general x7, matrix products, einsum(): return jnp.einsum(form, a.astype(jnp.float32), b.astype(jnp.float32))  305 us
    another operation x1, blocking collectives, placed(): return lax.with_sharding_constraint(v, NamedSharding(mesh, P(*spec)))  91.8 us
    another operation x1, waiting for transfers between devices, placed(): return lax.with_sharding_constraint(v, NamedSharding(mesh, P(*spec)))  84.6 us
  transfers between devices with their start and end apart: 1, of which 1 were waited for; matrix products, arithmetic and copies ran while one was open for 1% of the time, Pallas kernels for 0%

commit v1 on v0

v1 whole, which is shorter than its diff:
```python
import functools

import jax
import jax.numpy as jnp
from jax import lax
from jax.experimental import pallas as pl
from jax.experimental.pallas import tpu as pltpu
from jax.sharding import PartitionSpec as P

CHUNK = 16
ROWS = (256, 384, 512, 640)
TF = 512
TK = 1536
COLS = (768, 768, 768, 768)


def by_rows(total, rows, f):
    low = 0
    for m in rows:
        high = m // CHUNK
        pl.when((total > low) & (total <= high))(functools.partial(f, m))
        low = high


def up_kernel(slots, n_ref, off_ref, tot_ref, z_hbm, wg_ref, wu_ref, h_ref, z_ref, sem):
    e, j = pl.program_id(0), pl.program_id(1)
    devices = z_hbm.shape[0]

    def piece(k, s, q):
        row = pl.multiple_of(k * slots + q * CHUNK, CHUNK)
        to = pl.multiple_of((off_ref[k, s] + q) * CHUNK, CHUNK)
        return pltpu.make_async_copy(
            z_hbm.at[s, pl.ds(row, CHUNK), :], z_ref.at[k, pl.ds(to, CHUNK), :], sem.at[k]
        )

    @pl.when((e == 0) & (j == 0))
    def _():
        for k in range(2):
            for s in range(devices):
                @pl.loop(0, n_ref[k, s])
                def _(q):
                    piece(k, s, q).start()

            @pl.loop(tot_ref[k], z_ref.shape[1] // CHUNK)
            def _(q):
                to = pl.multiple_of(q * CHUNK, CHUNK)
                z_ref[k, pl.ds(to, CHUNK), :] = jnp.zeros((CHUNK, z_ref.shape[2]), z_ref.dtype)

    @pl.when(j == 0)
    def _():
        @pl.loop(0, tot_ref[e])
        def _(q):
            piece(e, 0, 0).wait()

    def compute(m):
        z = z_ref[e, :m, :]
        g = jnp.dot(z, wg_ref[0], preferred_element_type=jnp.float32)
        u = jnp.dot(z, wu_ref[0], preferred_element_type=jnp.float32)
        h_ref[0, :m, :] = (jax.nn.silu(g) * u).astype(h_ref.dtype)

    by_rows(tot_ref[e], ROWS, compute)


def down_kernel(slots, n_ref, off_ref, tot_ref, h_ref, w_ref, out_hbm, acc_ref, o_ref, zero_ref, sem):
    e, k = pl.program_id(0), pl.program_id(1)
    devices = out_hbm.shape[0]
    last = pl.num_programs(1) - 1
    per = slots // CHUNK

    @pl.when((e == 0) & (k == 0))
    def _():
        zero_ref[...] = jnp.zeros_like(zero_ref)

    def compute(m):
        part = jnp.dot(h_ref[0, :m, :], w_ref[0], preferred_element_type=jnp.float32)

        @pl.when(k == 0)
        def _():
            acc_ref[:m, :] = part

        @pl.when(k > 0)
        def _():
            acc_ref[:m, :] += part

    by_rows(tot_ref[e], ROWS, compute)

    def put(src, s, q):
        row = pl.multiple_of(e * slots + q * CHUNK, CHUNK)
        return pltpu.make_async_copy(src, out_hbm.at[s, pl.ds(row, CHUNK), :], sem)

    @pl.when(k == last)
    def _():
        o_ref[e] = acc_ref[...].astype(o_ref.dtype)
        for s in range(devices):
            @pl.loop(0, n_ref[e, s])
            def _(q):
                at = pl.multiple_of((off_ref[e, s] + q) * CHUNK, CHUNK)
                put(o_ref.at[e, pl.ds(at, CHUNK), :], s, q).start()

            @pl.loop(n_ref[e, s], per)
            def _(q):
                put(zero_ref, s, q).start()

        @pl.when(e == 1)
        def _():
            @pl.loop(0, 2 * devices * per)
            def _(q):
                put(zero_ref, 0, 0).wait()


def solution(mesh):
    devices = mesh.shape["ep"]

    def up(counts, z, w_gate, w_up, slots):
        held, d, ff = w_gate.shape
        rows = devices * slots
        return pl.pallas_call(
            functools.partial(up_kernel, slots),
            out_shape=jax.ShapeDtypeStruct((held, rows, ff), jnp.bfloat16),
            grid_spec=pltpu.PrefetchScalarGridSpec(
                num_scalar_prefetch=3,
                grid=(held, ff // TF),
                in_specs=[
                    pl.BlockSpec(memory_space=pl.ANY),
                    pl.BlockSpec((1, d, TF), lambda e, j, *_: (e, 0, j)),
                    pl.BlockSpec((1, d, TF), lambda e, j, *_: (e, 0, j)),
                ],
                out_specs=pl.BlockSpec((1, rows, TF), lambda e, j, *_: (e, 0, j)),
                scratch_shapes=[
                    pltpu.VMEM((held, rows, d), jnp.bfloat16),
                    pltpu.SemaphoreType.DMA((held,)),
                ],
            ),
            cost_estimate=pl.CostEstimate(
                flops=4 * held * rows * d * ff, bytes_accessed=4 * held * d * ff, transcendentals=0
            ),
            name="up",
        )(*counts, z, w_gate, w_up)

    def down(counts, h, w_down, slots, first, width):
        held, ff, d = w_down.shape
        rows = devices * slots
        at = first // width
        return pl.pallas_call(
            functools.partial(down_kernel, slots),
            out_shape=jax.ShapeDtypeStruct((devices, held * slots, width), jnp.bfloat16),
            grid_spec=pltpu.PrefetchScalarGridSpec(
                num_scalar_prefetch=3,
                grid=(held, ff // TK),
                in_specs=[
                    pl.BlockSpec((1, rows, TK), lambda e, k, *_: (e, 0, k)),
                    pl.BlockSpec((1, TK, width), lambda e, k, *_: (e, k, at)),
                ],
                out_specs=pl.BlockSpec(memory_space=pl.ANY),
                scratch_shapes=[
                    pltpu.VMEM((rows, width), jnp.float32),
                    pltpu.VMEM((held, rows, width), jnp.bfloat16),
                    pltpu.VMEM((CHUNK, width), jnp.bfloat16),
                    pltpu.SemaphoreType.DMA,
                ],
            ),
            cost_estimate=pl.CostEstimate(
                flops=2 * held * rows * width * ff, bytes_accessed=2 * held * width * ff, transcendentals=0
            ),
            name="down",
        )(*counts, h, w_down)

    def body(x, expert, slot, gate, w_gate, w_up, w_down):
        x, expert, slot, gate = x[0, 0], expert[0, 0], slot[0, 0], gate[0, 0]
        tokens, top = expert.shape
        held, d, ff = w_gate.shape
        experts = held * devices
        slots = 5 * tokens * top // (4 * experts)
        pos = jnp.where(slot < slots, expert * slots + slot, -1)
        weight = gate.astype(jnp.bfloat16).astype(jnp.float32)
        note = jnp.concatenate([pos.astype(jnp.float32), weight], axis=1)
        note = lax.all_gather(note, "ep")
        xs = lax.all_gather(x, "ep")
        here = held * slots
        pos = note[..., :top].astype(jnp.int32) - lax.axis_index("ep") * here
        weight = note[..., top:]
        hit = pos[..., None, :] == jnp.arange(here)[:, None]
        pick = jnp.any(hit, axis=-1).astype(jnp.bfloat16)
        combine = jnp.sum(jnp.where(hit, weight[..., None, :], 0.0), axis=-1).astype(jnp.bfloat16)
        ends = jnp.stack(
            [
                jnp.max(jnp.where((pos >= k * slots) & (pos < (k + 1) * slots), pos - k * slots + 1, 0), axis=(1, 2))
                for k in range(held)
            ]
        )
        n = (ends + CHUNK - 1) // CHUNK
        off = jnp.cumsum(n, axis=1) - n
        counts = (n, off, jnp.sum(n, axis=1))
        z = jnp.einsum("stc,std->scd", pick, xs, preferred_element_type=jnp.float32).astype(jnp.bfloat16)
        h = up(counts, z, w_gate, w_up, slots)
        first, parts = 0, []
        for width in COLS:
            out = down(counts, h, w_down, slots, first, width)
            part = jnp.einsum("stc,scd->std", combine, out, preferred_element_type=jnp.float32).astype(jnp.bfloat16)
            parts.append(lax.psum_scatter(part, "ep", scatter_dimension=0))
            first += width
        return jnp.concatenate(parts, axis=-1)[None, None]

    held = P("ep", None, None)
    own = P("dp", "ep", None, None)
    return jax.shard_map(
        body,
        mesh=mesh,
        in_specs=(own, own, own, own, held, held, held),
        out_specs=own,
        check_vma=False,
    )
```

time: 498 us -> 483 us (0.970)
  matrix products: 305 us -> 26.9 us
  Pallas kernels: 0 us -> 270 us
  blocking collectives: 91.8 us -> 14.2 us
  waiting for transfers between devices: 84.6 us -> 148 us
  between operations: 0.12 us -> 13.2 us
  local copies, waits for them, and re-layouts: 12.3 us -> 0.02 us
  other arithmetic: 0.01 us -> 9.37 us
    dot_general x7 -> x5, matrix products: 305 us -> 26.9 us  [the longest x4 17 us: body(): jnp.einsum('stc,scd->std', combine, out, preferred_element_type=jnp.float32)]
    pallas_call x0 -> x5, Pallas kernels: none -> 270 us  [the longest x1 150 us: up(): pl.pallas_call(functools.partial(up_kernel, slots), out_shape=jax.ShapeDt...]
    reduce_scatter x0 -> x4, waiting for transfers between devices: none -> 97 us  [body(): parts.append(lax.psum_scatter(part, 'ep', scatter_dimension=0))]
    another operation x1 -> x0, blocking collectives: 91.8 us -> none  [placed(): return lax.with_sharding_constraint(v, NamedSharding(mesh, P(*spec)))]
    another operation x1 -> x0, waiting for transfers between devices: 84.6 us -> none  [placed(): return lax.with_sharding_constraint(v, NamedSharding(mesh, P(*spec)))]
    all_gather x0 -> x1, waiting for transfers between devices: none -> 50.2 us  [body(): xs = lax.all_gather(x, 'ep')]
    all_gather x0 -> x1, blocking collectives: none -> 14.2 us  [body(): note = lax.all_gather(note, 'ep')]
    another operation x1 -> x0, local copies, waits for them, and re-layouts: 7.21 us -> none  [placed(): return lax.with_sharding_constraint(v, NamedSharding(mesh, P(*spec)))]
  transfers between devices with their start and end apart: 1 -> 5, of which waited for: 1 -> 4; matrix products, arithmetic and copies ran while one was open for 1% -> 4% of each run, Pallas kernels for 0% -> 19%
where the time goes in v1:
time: 483 us; the launch traced here: 482 us
  Pallas kernels  270 us (56%)
  waiting for transfers between devices  148 us (31%)
  matrix products  26.9 us (6%)
  blocking collectives  14.2 us (3%)
  between operations  13.2 us (3%)
  other arithmetic  9.37 us (2%)
    pallas_call x1, Pallas kernels, up(): pl.pallas_call(functools.partial(up_kernel, slots), out_shape=jax.ShapeDt...  150 us
    pallas_call x4, Pallas kernels, down(): pl.pallas_call(functools.partial(down_kernel, slots), out_shape=jax.Shape...  120 us
    reduce_scatter x4, waiting for transfers between devices, body(): parts.append(lax.psum_scatter(part, 'ep', scatter_dimension=0))  97 us
    all_gather x1, waiting for transfers between devices, body(): xs = lax.all_gather(x, 'ep')  50.2 us
    dot_general x4, matrix products, body(): jnp.einsum('stc,scd->std', combine, out, preferred_element_type=jnp.float32)  17 us
    all_gather x1, blocking collectives, body(): note = lax.all_gather(note, 'ep')  14.2 us
    dot_general x1, matrix products, body(): jnp.einsum('stc,std->scd', pick, xs, preferred_element_type=jnp.float32)  9.87 us
  transfers between devices with their start and end apart: 5, of which 4 were waited for; matrix products, arithmetic and copies ran while one was open for 4% of the time, Pallas kernels for 19%

profile of v1, /device:TPU:0, one launch (start us, length us, event | category | flops | bytes accessed | tf_op | source)
XLA Modules:
  0.0 482.0 jit_solution(8710546985467650378)
XLA Ops:
  6.5 0.7 all-gather.4.cloned.1.call-update
  7.3 0.0 reduce-scatter.5.cloned.1.call-start
  7.3 0.7 bitcast_convert_fusion
  8.0 0.7 convert_bitcast_fusion
  8.7 14.2 %all-gather = f32[2048,8]{0,1:T(8,128)S(1)} all-gather(f32[256,8]{0,1:T(8,128)S(1)} %pad_maximum_fusion), channel_id=2, replica_groups=mesh['dp'=1,'ep'=8] {'ep'}, dimensions={0}, use_global_device_ids=true | all-gather | bytes 73728 | tf_op jit(solution)/shard_map/all_gather | solution.py:177
  23.0 0.4 select_reduce_fusion.2
  23.4 0.7 fusion.7
  24.0 0.2 reduce_window_sum.11
  24.2 0.6 sub.24.off_ref
  24.8 1.7 fusion.5
  26.5 1.7 select_reduce_fusion
  28.3 50.2 %all-gather.4.cloned.1.call-done = bf16[8,1,256,3072]{3,2,1,0:T(8,128)(2,1)} async-done(((bf16[1,1,256,3072]{3,2,1,0:T(8,128)(2,1)}), bf16[8,1,256,3072]{3,2,1,0:T(8,128)(2,1)}) %all-gather.4.cloned.1.call-update) | async-done | bytes 12582928 | tf_op jit(solution)/shard_map/all_gather | solution.py:178
  78.5 9.9 %fusion.2.z_hbm = bf16[8,160,3072]{2,1,0:T(8,128)(2,1)} fusion(pred[8,256,160]{1,2,0:T(8,128)(4,1)S(1)} %fusion.5, bf16[8,1,256,3072]{3,2,1,0:T(8,128)(2,1)} %all-gather.4.cloned.1.call-done), kind=kOutput, calls=%fused_computation.2 | convolution fusion | flops 2017198080 | bytes 20774912 | tf_op jit(solution)/shard_map/stc,std->scd/dot_general | solution.py:194
  88.4 149.8 %up.1.h_ref = bf16[2,640,10752]{2,1,0:T(8,128)(2,1)} custom-call(s32[2,8]{1,0:T(2,128)} %copy-done.1, s32[2,8]{1,0:T(2,128)} %sub.24.off_ref, s32[2]{0:T(128)} %get-tuple-element.7.tot_ref, bf16[8,160,3072]{2,1,0:T(8,128)(2,1)} %fusion.2.z_hbm, bf16[2,3072,10752]{2,1,0:T(8,128)(2,1)} %wg_ref.1, bf16[2,3072,10752]{2,1,0:T(8,128)(2,1)} %wu_ref.1), custom_call_target="tpu_custom_call" | custom-call | flops 169114337280 | bytes 264241152 | tf_op jit(solution)/shard_map/up/pallas_call | solution.py:117
  238.2 30.2 %down.4 = bf16[8,160,768]{2,1,0:T(8,128)(2,1)} custom-call(s32[2,8]{1,0:T(2,128)} %copy-done.1, s32[2,8]{1,0:T(2,128)} %sub.24.off_ref, s32[2]{0:T(128)} %get-tuple-element.7.tot_ref, bf16[2,640,10752]{2,1,0:T(8,128)(2,1)} %up.1.h_ref, bf16[2,10752,3072]{2,1,0:T(8,128)(2,1)} %w_ref.7), custom_call_target="tpu_custom_call" | custom-call | flops 21139292160 | bytes 33030144 | tf_op jit(solution)/shard_map/down/pallas_call | solution.py:144
  268.4 4.4 convolution_convert_fusion.3
  272.8 0.0 reduce-scatter.5.cloned.1.call-update
  272.8 0.0 reduce-scatter.7.cloned.1.call-start
  272.9 29.9 %down.5 = bf16[8,160,768]{2,1,0:T(8,128)(2,1)} custom-call(s32[2,8]{1,0:T(2,128)} %copy-done.1, s32[2,8]{1,0:T(2,128)} %sub.24.off_ref, s32[2]{0:T(128)} %get-tuple-element.7.tot_ref, bf16[2,640,10752]{2,1,0:T(8,128)(2,1)} %up.1.h_ref, bf16[2,10752,3072]{2,1,0:T(8,128)(2,1)} %w_ref.7), custom_call_target="tpu_custom_call" | custom-call | flops 21139292160 | bytes 33030144 | tf_op jit(solution)/shard_map/down/pallas_call | solution.py:144
  302.8 4.2 convolution_convert_fusion.2
  307.0 0.0 reduce-scatter.7.cloned.1.call-update
  307.0 0.0 reduce-scatter.9.cloned.1.call-start
  307.1 30.0 %down.6 = bf16[8,160,768]{2,1,0:T(8,128)(2,1)} custom-call(s32[2,8]{1,0:T(2,128)} %copy-done.1, s32[2,8]{1,0:T(2,128)} %sub.24.off_ref, s32[2]{0:T(128)} %get-tuple-element.7.tot_ref, bf16[2,640,10752]{2,1,0:T(8,128)(2,1)} %up.1.h_ref, bf16[2,10752,3072]{2,1,0:T(8,128)(2,1)} %w_ref.7), custom_call_target="tpu_custom_call" | custom-call | flops 21139292160 | bytes 33030144 | tf_op jit(solution)/shard_map/down/pallas_call | solution.py:144
  337.0 4.2 convolution_convert_fusion.1
  341.3 0.0 reduce-scatter.11.cloned.1.call-start
  341.3 30.2 %down.7 = bf16[8,160,768]{2,1,0:T(8,128)(2,1)} custom-call(s32[2,8]{1,0:T(2,128)} %copy-done.1, s32[2,8]{1,0:T(2,128)} %sub.24.off_ref, s32[2]{0:T(128)} %get-tuple-element.7.tot_ref, bf16[2,640,10752]{2,1,0:T(8,128)(2,1)} %up.1.h_ref, bf16[2,10752,3072]{2,1,0:T(8,128)(2,1)} %w_ref.7), custom_call_target="tpu_custom_call" | custom-call | flops 21139292160 | bytes 33030144 | tf_op jit(solution)/shard_map/down/pallas_call | solution.py:144
  371.5 4.2 convolution_convert_fusion
  375.8 0.0 reduce-scatter.5.cloned.1.call-done
  375.8 15.6 %reduce-scatter.7.cloned.1.call-done = bf16[1,256,768]{2,1,0:T(8,128)(2,1)} async-done(((bf16[8,256,768]{2,1,0:T(8,128)(2,1)}), bf16[1,256,768]{2,1,0:T(8,128)(2,1)}) %reduce-scatter.7.cloned.1.call-update) | async-done | bytes 393232 | tf_op jit(solution)/shard_map/reduce_scatter | solution.py:200
  391.5 40.7 %reduce-scatter.9.cloned.1.call-done = bf16[1,256,768]{2,1,0:T(8,128)(2,1)} async-done(((bf16[8,256,768]{2,1,0:T(8,128)(2,1)}), bf16[1,256,768]{2,1,0:T(8,128)(2,1)}) %reduce-scatter.9.cloned.1.call-update) | async-done | bytes 393232 | tf_op jit(solution)/shard_map/reduce_scatter | solution.py:200
  432.2 40.7 %reduce-scatter.11.cloned.1.call-done = bf16[1,256,768]{2,1,0:T(8,128)(2,1)} async-done(((bf16[8,256,768]{2,1,0:T(8,128)(2,1)}), bf16[1,256,768]{2,1,0:T(8,128)(2,1)}) %reduce-scatter.11.cloned.1.call-update) | async-done | bytes 393232 | tf_op jit(solution)/shard_map/reduce_scatter | solution.py:200
  472.8 2.7 maximum_bitcast_fusion
  (9 shorter events, 0.1 us)
Async XLA Ops:
  6.5 71.9 %all-gather.4.cloned.1.call-start = ((), (), s32[]{:S(2)}) async-start(), calls=%async_computation.8 | async-start | bytes 14155776 | tf_op jit(solution)/shard_map/all_gather | solution.py:178
  7.3 368.6 %reduce-scatter.5.cloned.1.call-start = ((), (), s32[]{:S(2)}) async-start(), calls=%async_computation.4 | async-start | bytes 3538944 | tf_op jit(solution)/shard_map/reduce_scatter | solution.py:200
  24.0 64.3 %copy-start.1 = (s32[2,8]{1,0:T(2,128)}, s32[2,8]{1,0:T(2,128)S(1)}, u32[]{:S(2)}) copy-start(s32[2,8]{1,0:T(2,128)S(1)} %get-tuple-element.8.n_ref) | copy-start | bytes 196
  238.2 30.2 %copy-start = (bf16[8,256,160]{1,2,0:T(8,128)(2,1)S(1)}, bf16[8,256,160]{1,2,0:T(8,128)(2,1)}, u32[]{:S(2)}) copy-start(bf16[8,256,160]{1,2,0:T(8,128)(2,1)} %select_reduce_fusion) | copy-start | bytes 1966084
  272.8 118.7 %reduce-scatter.7.cloned.1.call-start = ((), (), s32[]{:S(2)}) async-start(), calls=%async_computation.5 | async-start | bytes 3538944 | tf_op jit(solution)/shard_map/reduce_scatter | solution.py:200
  307.0 125.1 %reduce-scatter.9.cloned.1.call-start = ((), (), s32[]{:S(2)}) async-start(), calls=%async_computation.6 | async-start | bytes 3538944 | tf_op jit(solution)/shard_map/reduce_scatter | solution.py:200
  341.3 131.6 %reduce-scatter.11.cloned.1.call-start = ((), (), s32[]{:S(2)}) async-start(), calls=%async_computation.7 | async-start | bytes 3538944 | tf_op jit(solution)/shard_map/reduce_scatter | solution.py:200
Sparse Core Ops, SparseCore 0:
  9.2 69.2 all-gather.3
  272.9 77.6 reduce-scatter.4
  353.9 37.5 reduce-scatter.6
  394.6 37.4 reduce-scatter.8
  435.3 37.4 reduce-scatter.10
